TPU v7x, 32 devices: a whole 2x2x4 slice. The times are simulated.
32 devices in a mesh: dp: 8 (over z, y), tensor: 4 (over x, core).
Axes of the slice: x: 2, y: 2, z: 4, core: 2. Of those that a mesh axis runs over, the one named last changes fastest.
Arguments:
- tokens: bfloat16 [12288, 1024], P('dp', 'tensor'), may hold values from -6 to 6
- segment_ids: int32 [12288], P('dp'), may hold values from 0 to 8, as said below
- w_query: bfloat16 [1024, 1024], P(None, 'tensor'), may hold values from -0.1875 to 0.1875
- w_key: bfloat16 [1024, 1024], P(None, 'tensor'), may hold values from -0.1875 to 0.1875
- w_value: bfloat16 [1024, 1024], P(None, 'tensor'), may hold values from -0.1875 to 0.1875
- b_query: bfloat16 [1024], P('tensor'), may hold values from -3 to 3
- b_value: bfloat16 [1024], P('tensor'), may hold values from -3 to 3
- w_out: bfloat16 [1024, 1024], P('tensor'), may hold values from -0.75 to 0.75
- b_out: bfloat16 [1024], P('tensor'), may hold values from -3 to 3
- gain_one: bfloat16 [1024], P('tensor'), may hold values from 0.5 to 1.5
- bias_one: bfloat16 [1024], P('tensor'), may hold values from -3 to 3
- w_in: bfloat16 [1024, 4096], P(None, 'tensor'), may hold values from -0.1875 to 0.1875
- b_in: bfloat16 [4096], P('tensor'), may hold values from -3 to 3
- w_down: bfloat16 [4096, 1024], P('tensor'), may hold values from -0.09375 to 0.09375
- b_down: bfloat16 [1024], P('tensor'), may hold values from -3 to 3
- gain_two: bfloat16 [1024], P('tensor'), may hold values from 0.5 to 1.5
- bias_two: bfloat16 [1024], P('tensor'), may hold values from -3 to 3
- cotangent: bfloat16 [12288, 1024], P('dp', 'tensor'), may hold values from -6 to 6
Outputs:
- out: bfloat16 [12288, 1024], P('dp', 'tensor')
- grad_tokens: bfloat16 [12288, 1024], P('dp', 'tensor')
- grad_w_query: float32 [1024, 1024], P(None, 'tensor')
- grad_w_key: float32 [1024, 1024], P(None, 'tensor')
- grad_w_value: float32 [1024, 1024], P(None, 'tensor')
- grad_b_query: float32 [1024], P('tensor')
- grad_b_value: float32 [1024], P('tensor')
- grad_w_out: float32 [1024, 1024], P('tensor')
- grad_b_out: float32 [1024], P('tensor')
- grad_gain_one: float32 [1024], P('tensor')
- grad_bias_one: float32 [1024], P('tensor')
- grad_w_in: float32 [1024, 4096], P(None, 'tensor')
- grad_b_in: float32 [4096], P('tensor')
- grad_w_down: float32 [4096, 1024], P('tensor')
- grad_b_down: float32 [1024], P('tensor')
- grad_gain_two: float32 [1024], P('tensor')
- grad_bias_two: float32 [1024], P('tensor')
Inputs may be any that keep to these rules, and one draw needn't show every extreme that they name: `segment_ids`: within each packed sequence of 512 tokens the ids run from 1 to 8 without falling, each id on at least one token, followed by one or more tail slots of id 0.
All inputs are finite; a program needn't handle non-finite values.
Results may differ from a plain program's by a relative error of at most 0.015.
Values may be sent and summed in bfloat16 or wider, within the bound.
No kernel may reach another device: no remote copies, remote signals or barrier semaphores. Data moves between devices by JAX's collectives and lax.ppermute only.
A program may use at most 128 MiB of HBM per device.

v0:
```python
import jax
import jax.numpy as jnp
from jax import lax
from jax.sharding import PartitionSpec as P

HD = 64
LEN = 512


epsilon = 1e-05
masked_fill = -1000000000.0


def over_rows(left, right):
    return lax.dot_general(
        left, right, (((0,), (0,)), ((), ())), preferred_element_type=jnp.float32
    )


def against(left, right):
    return lax.dot_general(
        left, right, (((1,), (1,)), ((), ())), preferred_element_type=jnp.float32
    )


def allowed_pairs(labels):
    length = labels.shape[0]
    same_label = labels[:, None] == labels[None, :]
    diagonal = lax.broadcasted_iota(jnp.int32, (length, length), 0) == lax.broadcasted_iota(
        jnp.int32, (length, length), 1
    )
    return same_label & ((labels[:, None] != 0) | diagonal)


def masked_scores(query_rows, key_rows, labels):
    score_scale = query_rows.shape[-1] ** (-0.5)
    scores = (
        jnp.einsum("qhd,khd->hqk", query_rows, key_rows, preferred_element_type=jnp.float32)
        * score_scale
    )
    return (jnp.where(allowed_pairs(labels)[None], scores, masked_fill), score_scale)


def attend_block(sliced):
    query_rows, key_rows, value_rows, labels = sliced
    scores, score_scale = masked_scores(query_rows, key_rows, labels)
    row_peak = jnp.max(scores, axis=-1, keepdims=True)
    exp_terms = jnp.exp(scores - row_peak)
    exp_total = jnp.sum(exp_terms, axis=-1, keepdims=True)
    probs = (exp_terms / exp_total).astype(jnp.bfloat16)
    context = jnp.einsum("hqk,khd->qhd", probs, value_rows, preferred_element_type=jnp.float32)
    return (context.astype(jnp.bfloat16), (row_peak + jnp.log(exp_total))[..., 0])


def attend_back(sliced):
    query_rows, key_rows, value_rows, labels, dcontext, log_total = sliced
    scores, score_scale = masked_scores(query_rows, key_rows, labels)
    probs = jnp.exp(scores - log_total[..., None])
    dprobs = jnp.einsum("qhd,khd->hqk", dcontext, value_rows, preferred_element_type=jnp.float32)
    row_delta = jnp.sum(probs * dprobs, axis=-1, keepdims=True)
    dscores = (probs * (dprobs - row_delta)).astype(jnp.bfloat16)
    dquery = (
        jnp.einsum("hqk,khd->qhd", dscores, key_rows, preferred_element_type=jnp.float32)
        * score_scale
    )
    dkey = (
        jnp.einsum("hqk,qhd->khd", dscores, query_rows, preferred_element_type=jnp.float32)
        * score_scale
    )
    dvalue = jnp.einsum(
        "hqk,qhd->khd", probs.astype(jnp.bfloat16), dcontext, preferred_element_type=jnp.float32
    )
    return (dquery.astype(jnp.bfloat16), dkey.astype(jnp.bfloat16), dvalue.astype(jnp.bfloat16))


def norm_from(values, row_sums, model_width):
    row_mean = row_sums[0] / model_width
    variance = row_sums[1] / model_width - row_mean * row_mean
    inv_std = lax.rsqrt(variance + epsilon)
    return ((values - row_mean[:, None]) * inv_std[:, None], inv_std)


def norm_back(scaled, normed, inv_std, row_sums, model_width):
    return inv_std[:, None] * (
        scaled - row_sums[0][:, None] / model_width - normed * row_sums[1][:, None] / model_width
    )


def summed(parts):
    return lax.psum(parts, "dp")


def local(
    tokens,
    segment_ids,
    w_query,
    w_key,
    w_value,
    b_query,
    b_value,
    w_out,
    b_out,
    gain_one,
    bias_one,
    w_in,
    b_in,
    w_down,
    b_down,
    gain_two,
    bias_two,
    cotangent,
):
    row_count = tokens.shape[0]
    model_width = w_query.shape[0]
    local_cols = w_query.shape[1]
    head_count = local_cols // HD
    seq_count = row_count // LEN
    proj_weight = jnp.concatenate([w_query, w_key, w_value], axis=1)
    proj_bias = jnp.concatenate(
        [
            b_query.astype(jnp.float32),
            jnp.zeros((local_cols,), jnp.float32),
            b_value.astype(jnp.float32),
        ]
    )
    inputs = lax.all_gather(tokens, "tensor", axis=1, tiled=True)
    projected = (
        jnp.dot(inputs, proj_weight, preferred_element_type=jnp.float32) + proj_bias
    ).astype(jnp.bfloat16)

    def heads_of(block):
        return block.reshape(seq_count, LEN, head_count, HD)

    queries = heads_of(projected[:, :local_cols])
    key_proj = heads_of(projected[:, local_cols : 2 * local_cols])
    value_proj = heads_of(projected[:, 2 * local_cols :])
    labels = segment_ids.reshape(seq_count, LEN)
    context, log_total = lax.map(attend_block, (queries, key_proj, value_proj, labels))
    context = context.reshape(row_count, local_cols)
    attn_mine = lax.psum_scatter(
        jnp.dot(context, w_out, preferred_element_type=jnp.float32),
        "tensor",
        scatter_dimension=1,
        tiled=True,
    )
    z_one = tokens.astype(jnp.float32) + attn_mine + b_out.astype(jnp.float32)
    sums_one = lax.psum((jnp.sum(z_one, axis=1), jnp.sum(z_one * z_one, axis=1)), "tensor")
    n_one, inv_one = norm_from(z_one, sums_one, model_width)
    h_one = n_one * gain_one.astype(jnp.float32) + bias_one.astype(jnp.float32)
    h_low = lax.all_gather(h_one.astype(jnp.bfloat16), "tensor", axis=1, tiled=True)
    pre_act = jnp.dot(h_low, w_in, preferred_element_type=jnp.float32) + b_in.astype(jnp.float32)
    hidden = jax.nn.gelu(pre_act, approximate=False).astype(jnp.bfloat16)
    feed_mine = lax.psum_scatter(
        jnp.dot(hidden, w_down, preferred_element_type=jnp.float32),
        "tensor",
        scatter_dimension=1,
        tiled=True,
    )
    z_two = h_one + feed_mine + b_down.astype(jnp.float32)
    sums_two = lax.psum((jnp.sum(z_two, axis=1), jnp.sum(z_two * z_two, axis=1)), "tensor")
    n_two, inv_two = norm_from(z_two, sums_two, model_width)
    result = (n_two * gain_two.astype(jnp.float32) + bias_two.astype(jnp.float32)).astype(
        jnp.bfloat16
    )
    grad_out = cotangent.astype(jnp.float32)
    grad_gain_two = jnp.sum(grad_out * n_two, axis=0)
    grad_bias_two = jnp.sum(grad_out, axis=0)
    scaled_two = grad_out * gain_two.astype(jnp.float32)
    back_two = lax.psum(
        (jnp.sum(scaled_two, axis=1), jnp.sum(scaled_two * n_two, axis=1)), "tensor"
    )
    dz_two = norm_back(scaled_two, n_two, inv_two, back_two, model_width)
    grad_b_down = jnp.sum(dz_two, axis=0)
    dz_two_low = lax.all_gather(dz_two.astype(jnp.bfloat16), "tensor", axis=1, tiled=True)
    grad_w_down = over_rows(hidden, dz_two_low)
    dhidden = against(dz_two_low, w_down)
    _, gelu_pull = jax.vjp(lambda value_in: jax.nn.gelu(value_in, approximate=False), pre_act)
    dpre = gelu_pull(dhidden)[0].astype(jnp.bfloat16)
    grad_w_in = over_rows(h_low, dpre)
    grad_b_in = jnp.sum(dpre.astype(jnp.float32), axis=0)
    dh_one = dz_two + lax.psum_scatter(
        against(dpre, w_in), "tensor", scatter_dimension=1, tiled=True
    )
    feed_grads = (grad_w_in, grad_b_in, grad_w_down, grad_b_down, grad_gain_two, grad_bias_two)
    grad_gain_one = jnp.sum(dh_one * n_one, axis=0)
    grad_bias_one = jnp.sum(dh_one, axis=0)
    scaled_one = dh_one * gain_one.astype(jnp.float32)
    back_one = lax.psum(
        (jnp.sum(scaled_one, axis=1), jnp.sum(scaled_one * n_one, axis=1)), "tensor"
    )
    dz_one = norm_back(scaled_one, n_one, inv_one, back_one, model_width)
    grad_b_out = jnp.sum(dz_one, axis=0)
    dz_one_low = lax.all_gather(dz_one.astype(jnp.bfloat16), "tensor", axis=1, tiled=True)
    grad_w_out = over_rows(context, dz_one_low)
    dcontext = heads_of(against(dz_one_low, w_out).astype(jnp.bfloat16))
    dquery, dkey, dvalue = lax.map(
        attend_back, (queries, key_proj, value_proj, labels, dcontext, log_total)
    )
    dprojected = jnp.concatenate(
        [
            dquery.reshape(row_count, local_cols),
            dkey.reshape(row_count, local_cols),
            dvalue.reshape(row_count, local_cols),
        ],
        axis=1,
    )
    grad_proj = over_rows(inputs, dprojected)
    grad_b_query = jnp.sum(dprojected[:, :local_cols].astype(jnp.float32), axis=0)
    grad_b_value = jnp.sum(dprojected[:, 2 * local_cols :].astype(jnp.float32), axis=0)
    input_part = lax.psum_scatter(
        against(dprojected, proj_weight).astype(jnp.bfloat16),
        "tensor",
        scatter_dimension=1,
        tiled=True,
    ).astype(jnp.float32)
    grad_tokens = (dz_one + input_part).astype(jnp.bfloat16)
    attention_grads = (
        grad_proj[:, :local_cols],
        grad_proj[:, local_cols : 2 * local_cols],
        grad_proj[:, 2 * local_cols :],
        grad_b_query,
        grad_b_value,
        grad_w_out,
        grad_b_out,
        grad_gain_one,
        grad_bias_one,
    )
    totals = tuple(summed(attention_grads + feed_grads))
    return (result, grad_tokens) + totals


def solution(mesh):
    placed = (
        P("dp", "tensor"),
        P("dp"),
        P(None, "tensor"),
        P(None, "tensor"),
        P(None, "tensor"),
        P("tensor"),
        P("tensor"),
        P("tensor", None),
        P("tensor"),
        P("tensor"),
        P("tensor"),
        P(None, "tensor"),
        P("tensor"),
        P("tensor", None),
        P("tensor"),
        P("tensor"),
        P("tensor"),
        P("dp", "tensor"),
    )
    return jax.shard_map(
        local,
        mesh=mesh,
        in_specs=placed,
        out_specs=(
            P("dp", "tensor"),
            P("dp", "tensor"),
            P(None, "tensor"),
            P(None, "tensor"),
            P(None, "tensor"),
            P("tensor"),
            P("tensor"),
            P("tensor", None),
            P("tensor"),
            P("tensor"),
            P("tensor"),
            P(None, "tensor"),
            P("tensor"),
            P("tensor", None),
            P("tensor"),
            P("tensor"),
            P("tensor"),
        ),
        check_vma=False,
    )
```

profile of v0, /device:TPU:0, one launch (start us, length us, event | category | flops | bytes accessed | tf_op | source)
XLA Modules:
  0.0 971.6 jit_solution(15447300485332187335)
XLA Ops:
  14.6 26.6 %all-gather.5.cloned.1.call-done = bf16[1536,1024]{1,0:T(8,128)(2,1)} async-done(((bf16[1536,256]{1,0:T(8,128)(2,1)}), bf16[1536,1024]{1,0:T(8,128)(2,1)}) %all-gather.5.cloned.1.call-update) | async-done | bytes 3145744 | tf_op jit(solution)/shard_map/all_gather | solution.py:126
  41.2 5.2 fusion.69
  50.4 3.6 reshape.227
  54.0 2.3 copy.54
  56.3 3.6 reshape.225
  59.9 2.3 copy.53
  63.1 18.4 %while.26 = (s32[]{:T(128)}, bf16[3,512,4,64]{1,3,2,0:T(8,128)(2,1)}, f32[3,4,512]{2,1,0:T(4,128)S(1)}, bf16[3,512,4,64]{1,3,2,0:T(8,128)(2,1)}, s32[3,512]{1,0:...) while((s32[]{:T(128)}, ...), condition=%wide.region_3.4_spmd, body=%wide.region_0.3_spmd.sunk | while | flops 282196480 | bytes 14756965 | solution.py:138
  66.2 3.0 fusion.140
  72.3 3.0 fusion.140
  78.4 3.0 fusion.140
  84.5 3.7 fusion.86
  88.9 57.4 %reduce-scatter.5.cloned.1.call-done = f32[1536,256]{1,0:T(8,128)} async-done(((f32[1536,1024]{1,0:T(8,128)}), f32[1536,256]{1,0:T(8,128)}) %reduce-scatter.5.cloned.1.call-update) | async-done | bytes 1572880 | tf_op jit(solution)/shard_map/reduce_scatter | solution.py:140
  146.3 3.0 fusion.79
  149.3 10.7 %all-reduce.5 = (f32[1536]{0:T(1024)S(1)}, f32[1536]{0:T(1024)S(1)}) all-reduce(f32[1536]{0:T(1024)S(1)} %get-tuple-element.191, f32[1536]{0:T(1024)S(1)} %get-tuple-element.190), channel_id=1, replica_groups=mesh['dp'=8,'tensor'=4] {'tensor'}, use_global_device_ids=true, to_apply=%region_8.9 | all-reduce | flops 3072 | bytes 24576 | tf_op jit(solution)/shard_map/psum | solution.py:147
  159.9 2.8 fusion.77
  162.8 29.6 %all-gather.7.cloned.1.call-done = bf16[1536,1024]{1,0:T(8,128)(2,1)} async-done(((bf16[1536,256]{1,0:T(8,128)(2,1)}), bf16[1536,1024]{1,0:T(8,128)(2,1)}) %all-gather.7.cloned.1.call-update) | async-done | bytes 3145744 | tf_op jit(solution)/shard_map/all_gather | solution.py:150
  192.4 19.5 %multiply_convert_fusion.1 = (bf16[1536,1024]{1,0:T(8,128)(2,1)S(1)}, f32[1536,1024]{1,0:T(8,128)}, f32[1536,1024]{1,0:T(8,128)}) fusion(f32[1024]{0:T(1024)S(1)} %convert_element_type.124, bf16[1536,1024]{1,0:T(8,128)(2,1)} %all-gather.7.cloned.1.call-done, bf16[1024,1024]{1,0:T(8,128)(2,1)S(1)} %copy-done), kind=kOutput, calls=%fused_computation.76 | convolution fusion | flops 3325034496 | bytes 20975616 | tf_op jit(solution)/shard_map/dot_general | solution.py:151
  213.7 5.3 fusion.87
  219.6 57.4 %reduce-scatter.7.cloned.1.call-done = f32[1536,256]{1,0:T(8,128)} async-done(((f32[1536,1024]{1,0:T(8,128)}), f32[1536,256]{1,0:T(8,128)}) %reduce-scatter.7.cloned.1.call-update) | async-done | bytes 1572880 | tf_op jit(solution)/shard_map/reduce_scatter | solution.py:153
  277.0 3.5 fusion.78
  280.5 10.1 %all-reduce.4 = (f32[1536]{0:T(1024)S(1)}, f32[1536]{0:T(1024)S(1)}) all-reduce(f32[1536]{0:T(1024)S(1)} %get-tuple-element.189, f32[1536]{0:T(1024)S(1)} %get-tuple-element.188), channel_id=1, replica_groups=mesh['dp'=8,'tensor'=4] {'tensor'}, use_global_device_ids=true, to_apply=%region_13.14 | all-reduce | flops 3072 | bytes 24576 | tf_op jit(solution)/shard_map/psum | solution.py:160
  290.7 2.6 fusion.76
  293.3 10.1 %all-reduce.3 = (f32[1536]{0:T(1024)S(1)}, f32[1536]{0:T(1024)S(1)}) all-reduce(f32[1536]{0:T(1024)S(1)} %get-tuple-element.185, f32[1536]{0:T(1024)S(1)} %get-tuple-element.192), channel_id=1, replica_groups=mesh['dp'=8,'tensor'=4] {'tensor'}, use_global_device_ids=true, to_apply=%region_17.18 | all-reduce | flops 3072 | bytes 24576 | tf_op jit(solution)/shard_map/psum | solution.py:169
  303.4 3.1 fusion.80
  308.9 29.4 %all-gather.9.cloned.1.call-done = bf16[1536,1024]{1,0:T(8,128)(2,1)} async-done(((bf16[1536,256]{1,0:T(8,128)(2,1)}), bf16[1536,1024]{1,0:T(8,128)(2,1)}) %all-gather.9.cloned.1.call-update) | async-done | bytes 3145744 | tf_op jit(solution)/shard_map/all_gather | solution.py:174
  338.3 11.8 %convert_reduce_fusion = (f32[1024]{0:T(1024)S(1)}, bf16[1536,1024]{1,0:T(8,128)(2,1)S(1)}) fusion(f32[1536,1024]{1,0:T(8,128)} %get-tuple-element.260, f32[1536,1024]{1,0:T(8,128)} %get-tuple-element.277, f32[1024]{0:T(1024)S(1)} %convert_element_type.124, bf16[1536,1024]{1,0:T(8,128)(2,1)} %all-gather.9.cloned.1.call-done, bf16[1024,1024]{1,0:T(8,128)(2,1)} %param.35), kind=kOutput, calls=%fused_computation.74 | convolution fusion | flops 3247963136 | bytes 20979712 | tf_op jit(solution)/shard_map/dot_general | solution.py:21
  351.8 5.6 fusion.88
  357.5 58.0 %reduce-scatter.9.cloned.1.call-done = f32[1536,256]{1,0:T(8,128)} async-done(((f32[1536,1024]{1,0:T(8,128)}), f32[1536,256]{1,0:T(8,128)}) %reduce-scatter.9.cloned.1.call-update) | async-done | bytes 1572880 | tf_op jit(solution)/shard_map/reduce_scatter | solution.py:181
  415.5 3.4 multiply_reduce_fusion.1
  418.9 10.1 %all-reduce.2 = (f32[1536]{0:T(1024)S(1)}, f32[1536]{0:T(1024)S(1)}) all-reduce(f32[1536]{0:T(1024)S(1)} %get-tuple-element.183, f32[1536]{0:T(1024)S(1)} %get-tuple-element.186), channel_id=1, replica_groups=mesh['dp'=8,'tensor'=4] {'tensor'}, use_global_device_ids=true, to_apply=%region_22.23 | all-reduce | flops 3072 | bytes 24576 | tf_op jit(solution)/shard_map/psum | solution.py:188
  429.0 2.3 fusion.82
  433.8 29.4 %all-gather.11.cloned.1.call-done = bf16[1536,1024]{1,0:T(8,128)(2,1)} async-done(((bf16[1536,256]{1,0:T(8,128)(2,1)}), bf16[1536,1024]{1,0:T(8,128)(2,1)}) %all-gather.11.cloned.1.call-update) | async-done | bytes 3145744 | tf_op jit(solution)/shard_map/all_gather | solution.py:193
  463.2 2.9 convolution_convert_fusion.1
  467.7 3.4 copy.60
  473.0 26.4 %while.27 = (s32[]{:T(128)}, bf16[3,512,4,64]{1,3,2,0:T(8,128)(2,1)}, bf16[3,512,4,64]{1,3,2,0:T(8,128)(2,1)}, bf16[3,512,4,64]{1,3,2,0:T(8,128)(2,1)S(1)}, bf16...) while((s32[]{:T(128)}, ...), condition=%wide.region_25.26_spmd, body=%wide.region_23.25_spmd.sunk | while | flops 688519680 | bytes 38344856 | solution.py:196
  475.4 2.5 multiply_reduce_fusion.7
  484.2 2.5 multiply_reduce_fusion.7
  493.0 2.5 multiply_reduce_fusion.7
  505.2 5.5 convolution_convert_fusion
  511.0 8.6 fusion.91
  519.6 5.0 fusion.90
  524.6 2.6 convolution_bitcast_fusion
  535.3 37.9 %all-reduce = (f32[256]{0:T(256)}, f32[256]{0:T(256)}, f32[256]{0:T(256)}, f32[256]{0:T(256)}, f32[256]{0:T(256)}, /*index=5*/f32[1024]{0:T(1024)}, f32[256]{0:T(256)}, f32[256]{0:T(256)}, f32[256]{0:T(256)}) all-reduce(f32[256]{0:T(256)S(1)} %reduce_sum.184, f32[256]{0:T(256)S(1)} %reduce_sum.186, ...), channel_id=1, replica_groups=mesh['dp'=8,'tensor'=4] {'dp'}, use_global_device_ids=true, to_apply=%region_31.32 | all-reduce | flops 3072 | bytes 24576 | tf_op jit(solution)/shard_map/psum | solution.py:90
  573.2 2.2 add_convert_fusion.2
  575.4 374.8 %all-reduce.8.cloned.1.call-done = (f32[1024,256]{0,1:T(8,128)}, f32[1024,256]{0,1:T(8,128)}, f32[1024,256]{0,1:T(8,128)}, f32[256,1024]{1,0:T(8,128)}, f32[1024,1024]{1,0:T(8,128)}, /*index=5*/f32[1024,1024]{1,0:T(8,128)}) async-done(((f32[1024,256]{0,1:T(8,128)}, f32[1024,256]{0,1:T(8,128)}, f32[1024,256]{0,1:T(8,128)}, f32[256,1024]{1,0:T(8,128)}, f32[1024,1024]{1,0:T(8,128)}, ...) | async-done | bytes 12582928 | tf_op jit(solution)/shard_map/psum | solution.py:90
  950.2 2.7 copy.65
  952.8 2.5 copy.66
  957.7 4.9 copy.117
  (185 shorter events, 74.8 us)
Async XLA Ops:
  7.2 185.2 %copy-start = (bf16[1024,1024]{1,0:T(8,128)(2,1)S(1)}, bf16[1024,1024]{1,0:T(8,128)(2,1)}, u32[]{:S(2)}) copy-start(bf16[1024,1024]{1,0:T(8,128)(2,1)} %param.33) | copy-start | bytes 6291460
  7.2 6.6 copy-start.17
  7.2 34.0 %all-gather.5.cloned.1.call-start = ((), (), s32[]{:S(2)}) async-start(), calls=%async_computation.4 | async-start | bytes 3932160 | tf_op jit(solution)/shard_map/all_gather | solution.py:126
  8.0 138.3 %reduce-scatter.5.cloned.1.call-start = ((), (), s32[]{:S(2)}) async-start(), calls=%async_computation.5 | async-start | bytes 7864320 | tf_op jit(solution)/shard_map/reduce_scatter | solution.py:140
  81.5 3.0 copy-start.16
  83.6 0.9 copy-start.10
  88.2 0.7 copy-start.25
  88.2 0.7 copy-start.26
  88.2 0.7 copy-start.27
  88.2 104.1 %all-gather.7.cloned.1.call-start = ((), (), s32[]{:S(2)}) async-start(), calls=%async_computation.6 | async-start | bytes 3932160 | tf_op jit(solution)/shard_map/all_gather | solution.py:150
  88.9 73.9 %copy-start.20 = (bf16[1024]{0:T(1024)(128)(2,1)S(1)}, bf16[1024]{0:T(1024)(128)(2,1)}, u32[]{:S(2)}) copy-start(bf16[1024]{0:T(1024)(128)(2,1)} %param.34) | copy-start | bytes 6148
  162.7 114.3 %reduce-scatter.7.cloned.1.call-start = ((), (), s32[]{:S(2)}) async-start(), calls=%async_computation.7 | async-start | bytes 7864320 | tf_op jit(solution)/shard_map/reduce_scatter | solution.py:153
  192.4 21.3 %copy-start.24 = (bf16[1024,1024]{1,0:T(8,128)(2,1)S(1)}, bf16[1024,1024]{1,0:T(8,128)(2,1)}, u32[]{:S(2)}) copy-start(bf16[1024,1024]{1,0:T(8,128)(2,1)} %param.35) | copy-start | bytes 6291460
  211.9 1.8 copy-start.31
  218.9 0.7 copy-start.28
  218.9 0.7 copy-start.29
  219.0 0.7 copy-start.30
  219.0 119.3 %all-gather.9.cloned.1.call-start = ((), (), s32[]{:S(2)}) async-start(), calls=%async_computation.8 | async-start | bytes 3932160 | tf_op jit(solution)/shard_map/all_gather | solution.py:174
  306.5 1.1 copy-start.6
  308.7 106.8 %reduce-scatter.9.cloned.1.call-start = ((), (), s32[]{:S(2)}) async-start(), calls=%async_computation.9 | async-start | bytes 7864320 | tf_op jit(solution)/shard_map/reduce_scatter | solution.py:181
  350.2 1.7 copy-start.32
  357.4 58.1 %copy-start.2 = (f32[1536,256]{1,0:T(8,128)S(1)}, f32[1536,256]{1,0:T(8,128)}, u32[]{:S(2)}) copy-start(f32[1536,256]{1,0:T(8,128)} %get-tuple-element.261) | copy-start | bytes 4718596
  357.4 105.7 %all-gather.11.cloned.1.call-start = ((), (), s32[]{:S(2)}) async-start(), calls=%async_computation.10 | async-start | bytes 3932160 | tf_op jit(solution)/shard_map/all_gather | solution.py:193
  431.3 1.2 copy-start.4
  433.5 139.6 %reduce-scatter.11.cloned.1.call-start = ((), (), s32[]{:S(2)}) async-start(), calls=%async_computation.11 | async-start | bytes 3932160 | tf_op jit(solution)/shard_map/reduce_scatter | solution.py:210
  466.1 6.9 copy-start.3
  473.0 1.1 copy-start.9
  481.8 1.1 copy-start.9
  490.6 1.1 copy-start.9
  499.4 3.2 copy-start.7
  501.5 1.2 copy-start.13
  503.7 1.4 copy-start.18
  510.7 439.5 %all-reduce.8.cloned.1.call-start = ((), (), s32[]{:S(2)}) async-start(), calls=%async_computation.12 | async-start | bytes 25165824 | tf_op jit(solution)/shard_map/psum | solution.py:90
  511.0 8.6 copy-start.22
  511.0 8.6 copy-start.33
  519.6 5.0 copy-start.19
  519.6 5.0 copy-start.21
  527.2 1.8 copy-start.11
  527.3 3.3 copy-start.23
  532.6 1.1 copy-start.8
  532.6 40.6 %copy-start.5 = (f32[1536,256]{1,0:T(8,128)S(1)}, f32[1536,256]{1,0:T(8,128)}, u32[]{:S(2)}) copy-start(f32[1536,256]{1,0:T(8,128)} %copy-done.4) | copy-start | bytes 4718596
  950.2 5.2 copy-start.15
  950.2 6.5 copy-start.14
  957.7 4.9 copy-start.12
  957.7 7.0 copy-start.1
Sparse Core Ops, SparseCore 0:
  9.6 31.6 all-gather.4
  88.4 57.8 reduce-scatter.4
  162.8 29.5 all-gather.6
  219.1 57.8 reduce-scatter.6
  308.8 29.4 all-gather.8
  357.5 57.8 reduce-scatter.8
  433.7 29.4 all-gather.10
  510.8 37.7 reduce-scatter.10
  555.1 394.9 all-reduce.7
where the time goes:
time: 981 us; the launch traced here: 972 us
  waiting for transfers between devices  663 us (68%)
  matrix products  114 us (12%)
  blocking collectives  79 us (8%)
  local copies, waits for them, and re-layouts  63.9 us (7%)
  other arithmetic  35.8 us (4%)
  between operations  14.7 us (1%)
    psum x1, waiting for transfers between devices, summed(): return lax.psum(parts, 'dp')  375 us
    reduce_scatter x1, waiting for transfers between devices, local(): lax.psum_scatter(against(dpre, w_in), 'tensor', scatter_dimension=1, tile...  58 us
    reduce_scatter x1, waiting for transfers between devices, local(): lax.psum_scatter(jnp.dot(hidden, w_down, preferred_element_type=jnp.float...  57.4 us
    reduce_scatter x1, waiting for transfers between devices, local(): lax.psum_scatter(jnp.dot(context, w_out, preferred_element_type=jnp.float...  57.4 us
    psum x1, blocking collectives, summed(): return lax.psum(parts, 'dp')  37.9 us
    unnamed x80, local copies, waits for them, and re-layouts  31.2 us
    all_gather x1, waiting for transfers between devices, local(): lax.all_gather(h_one.astype(jnp.bfloat16), 'tensor', axis=1, tiled=True)  29.6 us
    all_gather x1, waiting for transfers between devices, local(): lax.all_gather(dz_two.astype(jnp.bfloat16), 'tensor', axis=1, tiled=True)  29.4 us
  transfers between devices with their start and end apart: 9, of which 8 were waited for; matrix products, arithmetic and copies ran while one was open for 3% of the time, Pallas kernels for 0%

commit v1 on v0

v1 whole, which is shorter than its diff:
```python
import functools
import math

import jax
import jax.numpy as jnp
from jax import lax
from jax.experimental import pallas as pl
from jax.experimental.pallas import tpu as pltpu
from jax.sharding import PartitionSpec as P

HD = 64
LEN = 512
CHUNKS = (1, 1, 1)

EPSILON = 1e-05
MASKED = -1000000000.0
BF = jnp.bfloat16
F32 = jnp.float32


def mm(left, right):
    return lax.dot_general(left, right, (((1,), (0,)), ((), ())), preferred_element_type=F32)


def over_rows(left, right):
    return lax.dot_general(left, right, (((0,), (0,)), ((), ())), preferred_element_type=F32)


def against(left, right):
    return lax.dot_general(left, right, (((1,), (1,)), ((), ())), preferred_element_type=F32)


def swap(values, axis, bit):
    size = lax.axis_size(axis)
    return lax.ppermute(values, axis, [(i, i ^ bit) for i in range(size)])


def xor_order(blocks, t):
    odd = (t & 1) == 1
    upper = (t & 2) == 2
    b0, b1, b2, b3 = blocks
    q0, q1 = jnp.where(odd, b1, b0), jnp.where(odd, b0, b1)
    q2, q3 = jnp.where(odd, b3, b2), jnp.where(odd, b2, b3)
    return (
        jnp.where(upper, q2, q0),
        jnp.where(upper, q3, q1),
        jnp.where(upper, q0, q2),
        jnp.where(upper, q1, q3),
    )


def gather_blocks(own):
    across = swap(own, "tensor", 2)
    beside = swap(own, "tensor", 1)
    corner = swap(across, "tensor", 1)
    return own, beside, across, corner


def exchange_blocks(blocks):
    return (
        blocks[0],
        swap(blocks[1], "tensor", 1),
        swap(blocks[2], "tensor", 2),
        swap(blocks[3], "tensor", 3),
    )


def scatter_sum(blocks):
    b0, b1, b2, b3 = blocks
    far = swap(b3, "tensor", 1)
    near = swap(b1, "tensor", 1)
    onward = (b2.astype(F32) + far.astype(F32)).astype(BF)
    across = swap(onward, "tensor", 2)
    return (b0.astype(F32) + near.astype(F32)) + across.astype(F32)


def reduce_rows(values, bits, index):
    for bit in bits:
        half = values.shape[0] // 2
        mine = jnp.where((index & bit) == 0, 0, half)
        sent = lax.dynamic_slice_in_dim(values, half - mine, half, 0).astype(BF)
        kept = lax.dynamic_slice_in_dim(values, mine, half, 0)
        got = swap(sent, "dp", bit)
        values = kept.astype(F32) + got.astype(F32)
    return values.astype(BF)


def spread_rows(values, bits, index):
    for bit in reversed(bits):
        got = swap(values, "dp", bit)
        low = (index & bit) == 0
        values = jnp.concatenate([jnp.where(low, values, got), jnp.where(low, got, values)], axis=0)
    return values


def dp_bits(order):
    size = lax.axis_size("dp")
    bits = [1 << i for i in range(int(math.log2(size)))]
    turn = order % len(bits)
    return bits[turn:] + bits[:turn]


def summed_big(values, order, index):
    bits = dp_bits(order)
    return spread_rows(reduce_rows(values, bits, index), bits, index).astype(F32)


def summed_small(values):
    for bit in dp_bits(0):
        values = values + swap(values, "dp", bit)
    return values


def head_lanes(width, head):
    lane = lax.broadcasted_iota(jnp.int32, (1, width), 1)
    return (lane >= head * HD) & (lane < (head + 1) * HD)


def allowed_block(row_labels, column_labels):
    length = row_labels.shape[0]
    same = row_labels == column_labels
    diagonal = lax.broadcasted_iota(jnp.int32, (length, length), 0) == lax.broadcasted_iota(
        jnp.int32, (length, length), 1
    )
    return same & ((row_labels != 0) | diagonal)


def attend_kernel(q_ref, k_ref, v_ref, rows_ref, columns_ref, context_ref, total_ref):
    width = q_ref.shape[1]
    allowed = allowed_block(rows_ref[0], columns_ref[0])
    queries, keys, values = q_ref[...], k_ref[...], v_ref[...]
    context = jnp.zeros(q_ref.shape, F32)
    zero = jnp.zeros((), BF)
    for head in range(width // HD):
        lanes = head_lanes(width, head)
        scores = against(jnp.where(lanes, queries, zero), keys) * (HD**-0.5)
        scores = jnp.where(allowed, scores, MASKED)
        peak = jnp.max(scores, axis=1, keepdims=True)
        terms = jnp.exp(scores - peak)
        total = jnp.sum(terms, axis=1, keepdims=True)
        probs = (terms / total).astype(BF)
        context = context + mm(probs, jnp.where(lanes, values, zero))
        total_ref[0, :, head : head + 1] = peak + jnp.log(total)
    context_ref[...] = context.astype(BF)


def attend_back_kernel(
    q_ref, k_ref, v_ref, rows_ref, columns_ref, dcontext_ref, total_ref, out_ref
):
    width = q_ref.shape[1]
    allowed = allowed_block(rows_ref[0], columns_ref[0])
    queries, keys, values = q_ref[...], k_ref[...], v_ref[...]
    dcontext = dcontext_ref[...]
    scale = HD**-0.5
    dquery = jnp.zeros(q_ref.shape, F32)
    dkey = jnp.zeros(q_ref.shape, F32)
    dvalue = jnp.zeros(q_ref.shape, F32)
    zero = jnp.zeros((), BF)
    for head in range(width // HD):
        lanes = head_lanes(width, head)
        q_head = jnp.where(lanes, queries, zero)
        d_head = jnp.where(lanes, dcontext, zero)
        k_head = jnp.where(lanes, keys, zero)
        scores = against(q_head, keys) * scale
        scores = jnp.where(allowed, scores, MASKED)
        probs = jnp.exp(scores - total_ref[0, :, head : head + 1])
        dprobs = against(d_head, values)
        delta = jnp.sum(probs * dprobs, axis=1, keepdims=True)
        dscores = (probs * (dprobs - delta)).astype(BF)
        dquery = dquery + mm(dscores, k_head)
        dkey = dkey + over_rows(dscores, q_head)
        dvalue = dvalue + over_rows(probs.astype(BF), d_head)
    out_ref[:, :width] = (dquery * scale).astype(BF)
    out_ref[:, width : 2 * width] = (dkey * scale).astype(BF)
    out_ref[:, 2 * width :] = dvalue.astype(BF)


def sequence_specs(width):
    def third(part):
        return pl.BlockSpec((LEN, width), lambda s: (s, part))

    return [
        third(0),
        third(1),
        third(2),
        pl.BlockSpec((1, LEN, 1), lambda s: (s, 0, 0)),
        pl.BlockSpec((1, 1, LEN), lambda s: (s, 0, 0)),
    ]


def attend(projected, labels):
    rows, width = projected.shape[0], projected.shape[1] // 3
    count, heads = rows // LEN, width // HD
    return pl.pallas_call(
        attend_kernel,
        grid=(count,),
        in_specs=sequence_specs(width),
        out_specs=[
            pl.BlockSpec((LEN, width), lambda s: (s, 0)),
            pl.BlockSpec((1, LEN, heads), lambda s: (s, 0, 0)),
        ],
        out_shape=[
            jax.ShapeDtypeStruct((rows, width), BF),
            jax.ShapeDtypeStruct((count, LEN, heads), F32),
        ],
        cost_estimate=pl.CostEstimate(
            flops=count * 4 * LEN * LEN * width * heads,
            bytes_accessed=rows * width * 8,
            transcendentals=count * heads * LEN * LEN,
        ),
        name="attend",
    )(projected, projected, projected, labels[:, :, None], labels[:, None, :])


def attend_back(projected, labels, dcontext, log_total):
    rows, width = projected.shape[0], projected.shape[1] // 3
    count, heads = rows // LEN, width // HD
    return pl.pallas_call(
        attend_back_kernel,
        grid=(count,),
        in_specs=sequence_specs(width)
        + [
            pl.BlockSpec((LEN, width), lambda s: (s, 0)),
            pl.BlockSpec((1, LEN, heads), lambda s: (s, 0, 0)),
        ],
        out_specs=pl.BlockSpec((LEN, 3 * width), lambda s: (s, 0)),
        out_shape=jax.ShapeDtypeStruct((rows, 3 * width), BF),
        cost_estimate=pl.CostEstimate(
            flops=count * 10 * LEN * LEN * width * heads,
            bytes_accessed=rows * width * 14,
            transcendentals=count * heads * LEN * LEN,
        ),
        name="attend_back",
    )(
        projected,
        projected,
        projected,
        labels[:, :, None],
        labels[:, None, :],
        dcontext,
        log_total,
    )


def norm(values):
    center = values - jnp.mean(values, axis=1, keepdims=True)
    inverse = lax.rsqrt(jnp.mean(center * center, axis=1, keepdims=True) + EPSILON)
    return center * inverse, inverse


def norm_back(scaled, normed, inverse):
    mean = jnp.mean(scaled, axis=1, keepdims=True)
    along = jnp.mean(scaled * normed, axis=1, keepdims=True)
    return inverse * (scaled - mean - normed * along)


def gelu_both(pre_act):
    cdf = 0.5 * (1.0 + lax.erf(pre_act * (2.0**-0.5)))
    slope = cdf + pre_act * jnp.exp(-0.5 * pre_act * pre_act) * ((2.0 * math.pi) ** -0.5)
    return (pre_act * cdf).astype(BF), slope.astype(BF)


def total_of(parts):
    return functools.reduce(lambda a, b: a + b, parts)


def local(
    tokens,
    segment_ids,
    w_query,
    w_key,
    w_value,
    b_query,
    b_value,
    w_out,
    b_out,
    gain_one,
    bias_one,
    w_in,
    b_in,
    w_down,
    b_down,
    gain_two,
    bias_two,
    cotangent,
):
    t = lax.axis_index("tensor")
    d = lax.axis_index("dp")
    ways = 4
    row_count = tokens.shape[0]
    width = w_query.shape[0]
    cols = w_query.shape[1]
    sequences = row_count // LEN
    chunks = CHUNKS if sum(CHUNKS) == sequences else (sequences,)
    labels = segment_ids.reshape(sequences, LEN)

    def blocks_of(values, axis=0):
        return jnp.split(values, ways, axis=axis)

    def rows_rel(values):
        r = values.shape[0] // ways
        return [lax.dynamic_slice_in_dim(values, (t ^ k) * r, r, 0) for k in range(ways)]

    vectors = jnp.stack([b_out, gain_one, bias_one, b_down, gain_two, bias_two])
    vectors = jnp.concatenate(xor_order(gather_blocks(vectors), t), axis=1).astype(F32)
    b_out_f, gain_one_f, bias_one_f, b_down_f, gain_two_f, bias_two_f = (
        vectors[i : i + 1] for i in range(6)
    )
    proj_weight = jnp.concatenate([w_query, w_key, w_value], axis=1)
    proj_bias = jnp.concatenate([b_query.astype(F32), jnp.zeros((cols,), F32), b_value.astype(F32)])
    weight_rel = jnp.concatenate(rows_rel(proj_weight), axis=0)

    first = 0
    spans = []
    for count in chunks:
        spans.append((first, count))
        first += count

    xs, projs, ctxs, totals, z_ones = [], [], [], [], []
    for start, count in spans:
        mine = tokens[start * LEN : (start + count) * LEN]
        xs.append(jnp.concatenate(xor_order(gather_blocks(mine), t), axis=1))
    cots = []
    for start, count in spans:
        mine = cotangent[start * LEN : (start + count) * LEN]
        cots.append(jnp.concatenate(xor_order(exchange_blocks(rows_rel(mine)), t), axis=1))

    h_ones, n_ones, inv_ones, h_rels = [], [], [], []
    for i, (start, count) in enumerate(spans):
        proj = (mm(xs[i], proj_weight) + proj_bias).astype(BF)
        context, log_total = attend(proj, labels[start : start + count])
        ctx_rel = jnp.concatenate(rows_rel(context), axis=0)
        part = mm(ctx_rel, w_out).astype(BF)
        attn = scatter_sum(blocks_of(part))
        r = count * LEN // ways
        x_mine = lax.dynamic_slice_in_dim(xs[i], t * r, r, 0)
        z_one = x_mine.astype(F32) + attn + b_out_f
        n_one, inv_one = norm(z_one)
        h_one = n_one * gain_one_f + bias_one_f
        projs.append(proj)
        ctxs.append(ctx_rel)
        totals.append(log_total)
        h_ones.append(h_one)
        n_ones.append(n_one)
        inv_ones.append(inv_one)
        h_rels.append(jnp.concatenate(gather_blocks(h_one.astype(BF)), axis=0))

    outs, dz_twos, dz_rels, hiddens, slopes = [], [], [], [], []
    gain_two_parts, bias_two_parts, b_down_parts = [], [], []
    for i, (start, count) in enumerate(spans):
        pre_act = mm(h_rels[i], w_in) + b_in.astype(F32)
        hidden, slope = gelu_both(pre_act)
        part = mm(hidden, w_down).astype(BF)
        z_two = h_ones[i] + scatter_sum(blocks_of(part)) + b_down_f
        n_two, inv_two = norm(z_two)
        result = (n_two * gain_two_f + bias_two_f).astype(BF)
        grad_out = cots[i].astype(F32)
        gain_two_parts.append(jnp.sum(grad_out * n_two, axis=0))
        bias_two_parts.append(jnp.sum(grad_out, axis=0))
        dz_two = norm_back(grad_out * gain_two_f, n_two, inv_two)
        b_down_parts.append(jnp.sum(dz_two, axis=0))
        dz_twos.append(dz_two)
        hiddens.append(hidden)
        slopes.append(slope)
        dz_rels.append(jnp.concatenate(gather_blocks(dz_two.astype(BF)), axis=0))
        rel_cols = [
            lax.dynamic_slice_in_dim(result, (t ^ k) * cols, cols, 1) for k in range(ways)
        ]
        outs.append(jnp.concatenate(xor_order(exchange_blocks(rel_cols), t), axis=0))

    dz_ones, dz1_rels, dpres = [], [], []
    gain_one_parts, bias_one_parts, b_out_parts, b_in_parts = [], [], [], []
    for i, (start, count) in enumerate(spans):
        dhidden = against(dz_rels[i], w_down)
        dpre = (dhidden * slopes[i].astype(F32)).astype(BF)
        b_in_parts.append(jnp.sum(dpre.astype(F32), axis=0))
        part = against(dpre, w_in).astype(BF)
        dh_one = dz_twos[i] + scatter_sum(blocks_of(part))
        gain_one_parts.append(jnp.sum(dh_one * n_ones[i], axis=0))
        bias_one_parts.append(jnp.sum(dh_one, axis=0))
        dz_one = norm_back(dh_one * gain_one_f, n_ones[i], inv_ones[i])
        b_out_parts.append(jnp.sum(dz_one, axis=0))
        dpres.append(dpre)
        dz1_rels.append(jnp.concatenate(gather_blocks(dz_one.astype(BF)), axis=0))

    def all_rows(parts):
        return parts[0] if len(parts) == 1 else jnp.concatenate(parts, axis=0)

    grad_w_down = summed_big(over_rows(all_rows(hiddens), all_rows(dz_rels)), 0, d)
    grad_w_in = summed_big(over_rows(all_rows(h_rels), all_rows(dpres)), 1, d)

    grad_tokens, dprojs = [], []
    for i, (start, count) in enumerate(spans):
        dcontext = against(dz1_rels[i], w_out).astype(BF)
        dcontext = jnp.concatenate(rows_rel(dcontext), axis=0)
        dproj = attend_back(projs[i], labels[start : start + count], dcontext, totals[i])
        dprojs.append(dproj)
        part = against(dproj, weight_rel).astype(BF)
        dz_cols = lax.dynamic_slice_in_dim(dz1_rels[i], t * cols, cols, 1)
        dz_cols = jnp.concatenate(rows_rel(dz_cols), axis=0)
        summed = scatter_sum(blocks_of(part, axis=1))
        grad_tokens.append((dz_cols.astype(F32) + summed).astype(BF))

    grad_w_out = summed_big(over_rows(all_rows(ctxs), all_rows(dz1_rels)), 0, d)
    dproj_all = all_rows(dprojs)
    grad_proj = summed_big(over_rows(all_rows(xs), dproj_all), 1, d)
    b_proj = jnp.sum(dproj_all.astype(F32), axis=0).reshape(3, cols)

    wide = jnp.stack(
        [
            total_of(p)
            for p in (
                gain_two_parts,
                bias_two_parts,
                b_down_parts,
                gain_one_parts,
                bias_one_parts,
                b_out_parts,
            )
        ]
    )
    wide_rel = [lax.dynamic_slice_in_dim(wide, (t ^ k) * cols, cols, 1) for k in range(ways)]
    narrow = total_of(exchange_blocks(wide_rel))
    b_in_sum = total_of(b_in_parts).reshape(-1, cols)
    small = summed_small(jnp.concatenate([narrow, b_in_sum], axis=0))
    b_proj = summed_small(b_proj)

    return (
        all_rows(outs),
        all_rows(grad_tokens),
        grad_proj[:, :cols],
        grad_proj[:, cols : 2 * cols],
        grad_proj[:, 2 * cols :],
        b_proj[0],
        b_proj[2],
        grad_w_out,
        small[5],
        small[3],
        small[4],
        grad_w_in,
        small[6:].reshape(-1),
        grad_w_down,
        small[2],
        small[0],
        small[1],
    )


def solution(mesh):
    placed = (
        P("dp", "tensor"),
        P("dp"),
        P(None, "tensor"),
        P(None, "tensor"),
        P(None, "tensor"),
        P("tensor"),
        P("tensor"),
        P("tensor", None),
        P("tensor"),
        P("tensor"),
        P("tensor"),
        P(None, "tensor"),
        P("tensor"),
        P("tensor", None),
        P("tensor"),
        P("tensor"),
        P("tensor"),
        P("dp", "tensor"),
    )
    return jax.shard_map(
        local,
        mesh=mesh,
        in_specs=placed,
        out_specs=(
            P("dp", "tensor"),
            P("dp", "tensor"),
            P(None, "tensor"),
            P(None, "tensor"),
            P(None, "tensor"),
            P("tensor"),
            P("tensor"),
            P("tensor", None),
            P("tensor"),
            P("tensor"),
            P("tensor"),
            P(None, "tensor"),
            P("tensor"),
            P("tensor", None),
            P("tensor"),
            P("tensor"),
            P("tensor"),
        ),
        check_vma=False,
    )
```

time: 981 us -> 523 us (0.53)
  waiting for transfers between devices: 663 us -> 224 us
  starting transfers between devices: 1.01 us -> 83.6 us
  blocking collectives: 79 us -> 0 us
  matrix products: 114 us -> 60.5 us
  Pallas kernels: 0 us -> 33.4 us
  other arithmetic: 35.8 us -> 49.3 us
  between operations: 14.7 us -> 3.52 us
    psum x1 -> x0, waiting for transfers between devices: 375 us -> none  [summed(): return lax.psum(parts, 'dp')]
    ppermute x0 -> x126, waiting for transfers between devices: none -> 224 us  [swap(): return lax.ppermute(values, axis, [(i, i ^ bit) for i in range(size)])]
    reduce_scatter x4 -> x0, waiting for transfers between devices: 173 us -> none  [the longest x1 58 us: local(): lax.psum_scatter(against(dpre, w_in), 'tensor', scatter_dimension=1, tile...]
    all_gather x4 -> x0, waiting for transfers between devices: 115 us -> none  [the longest x1 29.6 us: local(): lax.all_gather(h_one.astype(jnp.bfloat16), 'tensor', axis=1, tiled=True)]
    ppermute x0 -> x126, starting transfers between devices: none -> 83.6 us  [swap(): return lax.ppermute(values, axis, [(i, i ^ bit) for i in range(size)])]
    psum x5 -> x0, blocking collectives: 79 us -> none  [the longest x1 37.9 us: summed(): return lax.psum(parts, 'dp')]
    dot_general x25 -> x12, matrix products: 69.8 us -> 18.5 us  [mm(): lax.dot_general(left, right, (((1,), (0,)), ((), ())), preferred_element_...]
    pallas_call x0 -> x6, Pallas kernels: none -> 33.4 us  [the longest x3 19.4 us: attend_back(): pl.pallas_call(attend_back_kernel, grid=(count,), in_specs=sequence_specs...]
  transfers between devices with their start and end apart: 9 -> 126, of which waited for: 8 -> 49; matrix products, arithmetic and copies ran while one was open for 3% -> 25% of each run, Pallas kernels for 0% -> 5%
where the time goes in v1:
time: 523 us; the launch traced here: 513 us
  waiting for transfers between devices  224 us (43%)
  starting transfers between devices  83.6 us (16%)
  matrix products  60.5 us (12%)
  local copies, waits for them, and re-layouts  58.7 us (11%)
  other arithmetic  49.3 us (9%)
  Pallas kernels  33.4 us (6%)
    ppermute x126, waiting for transfers between devices, swap(): return lax.ppermute(values, axis, [(i, i ^ bit) for i in range(size)])  224 us
    ppermute x126, starting transfers between devices, swap(): return lax.ppermute(values, axis, [(i, i ^ bit) for i in range(size)])  83.6 us
    unnamed x276, local copies, waits for them, and re-layouts  28.4 us
    dot_general x12, matrix products, against(): lax.dot_general(left, right, (((1,), (1,)), ((), ())), preferred_element_...  23 us
    pallas_call x3, Pallas kernels, attend_back(): pl.pallas_call(attend_back_kernel, grid=(count,), in_specs=sequence_specs...  19.4 us
    dot_general x4, matrix products, over_rows(): lax.dot_general(left, right, (((0,), (0,)), ((), ())), preferred_element_...  19 us
    dot_general x12, matrix products, mm(): lax.dot_general(left, right, (((1,), (0,)), ((), ())), preferred_element_...  18.5 us
    pallas_call x3, Pallas kernels, attend(): pl.pallas_call(attend_kernel, grid=(count,), in_specs=sequence_specs(widt...  14 us
  transfers between devices with their start and end apart: 126, of which 49 were waited for; matrix products, arithmetic and copies ran while one was open for 25% of the time, Pallas kernels for 5%

profile of v1, /device:TPU:0, one launch (start us, length us, event | category | flops | bytes accessed | tf_op | source)
XLA Modules:
  0.0 512.6 jit_solution(10312337384133989656)
XLA Ops:
  19.9 2.7 constant_dynamic-slice_fusion.21
  46.0 4.3 collective-permute-done
  50.5 5.5 %collective-permute-done.18 = bf16[512,256]{1,0:T(8,128)(2,1)} collective-permute-done((bf16[512,256]{1,0:T(8,128)(2,1)}, bf16[512,256]{1,0:T(8,128)(2,1)}, u32[]{:S(2)}, u32[]{:S(2)}) %collective-permute-start.18) | collective-permute-done | bytes 262176 | tf_op jit(solution)/shard_map/ppermute | solution.py:35
  57.9 4.6 attend.5
  67.6 4.6 attend.3
  78.2 3.3 add_convert_fusion.1.q_ref.k_ref.v_ref
  81.5 4.8 attend.4
  103.3 5.3 %collective-permute-done.38 = bf16[128,1024]{1,0:T(8,128)(2,1)S(1)} collective-permute-done((bf16[128,1024]{1,0:T(8,128)(2,1)S(1)}, bf16[128,1024]{1,0:T(8,128)(2,1)S(1)}, u32[]{:S(2)}, u32[]{:S(2)}) %collective-permute-start.38) | collective-permute-done | bytes 262176 | tf_op jit(solution)/shard_map/ppermute | solution.py:35
  108.6 5.6 %collective-permute-done.23 = bf16[128,1024]{1,0:T(8,128)(2,1)S(1)} collective-permute-done((bf16[128,1024]{1,0:T(8,128)(2,1)S(1)}, bf16[128,1024]{1,0:T(8,128)(2,1)S(1)}, u32[]{:S(2)}, u32[]{:S(2)}) %collective-permute-start.23) | collective-permute-done | bytes 262176 | tf_op jit(solution)/shard_map/ppermute | solution.py:35
  114.2 5.0 collective-permute-done.5
  120.8 7.1 %collective-permute-done.10 = bf16[128,1024]{1,0:T(8,128)(2,1)S(1)} collective-permute-done((bf16[128,1024]{1,0:T(8,128)(2,1)S(1)}, bf16[128,1024]{1,0:T(8,128)(2,1)S(1)}, u32[]{:S(2)}, u32[]{:S(2)}) %collective-permute-start.10) | collective-permute-done | bytes 262176 | tf_op jit(solution)/shard_map/ppermute | solution.py:35
  130.4 7.8 %collective-permute-done.25 = bf16[128,1024]{1,0:T(8,128)(2,1)S(1)} collective-permute-done((bf16[128,1024]{1,0:T(8,128)(2,1)S(1)}, bf16[128,1024]{1,0:T(8,128)(2,1)S(1)}, u32[]{:S(2)}, u32[]{:S(2)}) %collective-permute-start.25) | collective-permute-done | bytes 262176 | tf_op jit(solution)/shard_map/ppermute | solution.py:35
  141.7 6.6 %collective-permute-done.40 = bf16[128,1024]{1,0:T(8,128)(2,1)S(1)} collective-permute-done((bf16[128,1024]{1,0:T(8,128)(2,1)S(1)}, bf16[128,1024]{1,0:T(8,128)(2,1)S(1)}, u32[]{:S(2)}, u32[]{:S(2)}) %collective-permute-start.40) | collective-permute-done | bytes 262176 | tf_op jit(solution)/shard_map/ppermute | solution.py:35
  162.0 6.5 %collective-permute-done.14 = bf16[128,1024]{1,0:T(8,128)(2,1)S(1)} collective-permute-done((bf16[128,1024]{1,0:T(8,128)(2,1)S(1)}, bf16[128,1024]{1,0:T(8,128)(2,1)S(1)}, u32[]{:S(2)}, u32[]{:S(2)}) %collective-permute-start.14) | collective-permute-done | bytes 262176 | tf_op jit(solution)/shard_map/ppermute | solution.py:35
  170.1 4.0 collective-permute-done.44
  174.1 5.6 %collective-permute-done.29 = bf16[128,1024]{1,0:T(8,128)(2,1)S(1)} collective-permute-done((bf16[128,1024]{1,0:T(8,128)(2,1)S(1)}, bf16[128,1024]{1,0:T(8,128)(2,1)S(1)}, u32[]{:S(2)}, u32[]{:S(2)}) %collective-permute-start.29) | collective-permute-done | bytes 262176 | tf_op jit(solution)/shard_map/ppermute | solution.py:35
  191.9 3.9 collective-permute-done.46
  199.2 4.0 convert_reduce_fusion.3
  209.4 3.1 convert_reduce_fusion.2
  218.4 3.2 convert_reduce_fusion.1
  223.1 5.1 fusion.30
  229.6 5.4 %fusion.24 = f32[1024,1024]{1,0:T(8,128)} fusion(bf16[1536,1024]{1,0:T(8,128)(2,1)S(1)} %constant_dynamic-update-slice_fusion.39, bf16[512,1024]{1,0:T(8,128)(2,1)S(1)} %get-tuple-element.300, bf16[512,1024]{1,0:T(8,128)(2,1)S(1)} %get-tuple-element.304, bf16[512,1024]{1,0:T(8,128)(2,1)S(1)} %get-tuple-element.302), kind=kOutput, calls=%fused_computation.25 | convolution fusion | flops 3230662656 | bytes 10485760 | tf_op jit(solution)/shard_map/dot_general | solution.py:26
  237.8 5.4 %collective-permute-done.56 = bf16[128,1024]{1,0:T(8,128)(2,1)S(1)} collective-permute-done((bf16[128,1024]{1,0:T(8,128)(2,1)S(1)}, bf16[128,1024]{1,0:T(8,128)(2,1)S(1)}, u32[]{:S(2)}, u32[]{:S(2)}) %collective-permute-start.56) | collective-permute-done | bytes 262176 | tf_op jit(solution)/shard_map/ppermute | solution.py:35
  258.2 18.8 %collective-permute-done.112 = f32[10,256]{1,0:T(8,128)S(1)} collective-permute-done((f32[10,256]{1,0:T(8,128)S(1)}, f32[10,256]{1,0:T(8,128)S(1)}, u32[]{:S(2)}, u32[]{:S(2)}) %collective-permute-start.112) | collective-permute-done | bytes 10272 | tf_op jit(solution)/shard_map/ppermute | solution.py:35
  277.1 2.6 collective-permute-start.113
  282.9 3.2 collective-permute-done.58
  292.4 6.4 %attend_back.3 = bf16[512,768]{1,0:T(8,128)(2,1)} custom-call(bf16[512,768]{1,0:T(8,128)(2,1)} %add_convert_fusion.2.q_ref.k_ref.v_ref, bf16[512,768]{1,0:T(8,128)(2,1)} %add_convert_fusion.2.q_ref.k_ref.v_ref, bf16[512,768]{1,0:T(8,128)(2,1)} %add_convert_fusion.2.q_ref.k_ref.v_ref, s32[1,512,1]{2,1,0:T(8,128)} %copy.35.rows_ref, s32[1,1,512]{2,1,0:T(1,128)} %bitcast.102, ...), custom_call_target="tpu_custom_call" | custom-call | flops 2684354560 | bytes 1835008 | tf_op jit(solution)/shard_map/attend_back/pallas_call | solution.py:218
  298.8 2.6 convolution_convert_fusion.2
  315.7 6.5 %attend_back.4 = bf16[512,768]{1,0:T(8,128)(2,1)} custom-call(bf16[512,768]{1,0:T(8,128)(2,1)} %add_convert_fusion.1.q_ref.k_ref.v_ref, bf16[512,768]{1,0:T(8,128)(2,1)} %add_convert_fusion.1.q_ref.k_ref.v_ref, bf16[512,768]{1,0:T(8,128)(2,1)} %add_convert_fusion.1.q_ref.k_ref.v_ref, s32[1,512,1]{2,1,0:T(8,128)} %copy.36.rows_ref, s32[1,1,512]{2,1,0:T(1,128)} %bitcast.99, ...), custom_call_target="tpu_custom_call" | custom-call | flops 2684354560 | bytes 1835008 | tf_op jit(solution)/shard_map/attend_back/pallas_call | solution.py:218
  322.3 2.6 convolution_convert_fusion.1
  331.2 2.7 collective-permute-done.116
  334.6 7.1 %collective-permute-done.122 = bf16[128,1024]{1,0:T(8,128)(2,1)S(1)} collective-permute-done((bf16[128,1024]{1,0:T(8,128)(2,1)S(1)}, bf16[128,1024]{1,0:T(8,128)(2,1)S(1)}, u32[]{:S(2)}, u32[]{:S(2)}) %collective-permute-start.122) | collective-permute-done | bytes 262176 | tf_op jit(solution)/shard_map/ppermute | solution.py:35
  351.1 6.5 %attend_back.5 = bf16[512,768]{1,0:T(8,128)(2,1)} custom-call(bf16[512,768]{1,0:T(8,128)(2,1)} %add_convert_fusion.q_ref.k_ref.v_ref, bf16[512,768]{1,0:T(8,128)(2,1)} %add_convert_fusion.q_ref.k_ref.v_ref, bf16[512,768]{1,0:T(8,128)(2,1)} %add_convert_fusion.q_ref.k_ref.v_ref, s32[1,512,1]{2,1,0:T(8,128)} %copy.37.rows_ref, s32[1,1,512]{2,1,0:T(1,128)} %bitcast.96, ...), custom_call_target="tpu_custom_call" | custom-call | flops 2684354560 | bytes 1835008 | tf_op jit(solution)/shard_map/attend_back/pallas_call | solution.py:218
  357.7 6.3 %fusion = f32[1024,768]{1,0:T(8,128)} fusion(bf16[512,256]{1,0:T(8,128)(2,1)S(1)} %copy-done.45, bf16[512,256]{1,0:T(8,128)(2,1)S(1)} %copy-done.42, bf16[512,256]{1,0:T(8,128)(2,1)S(1)} %copy-done.39, bf16[512,256]{1,0:T(8,128)(2,1)S(1)} %copy-done.36, bf16[512,256]{1,0:T(8,128)(2,1)S(1)} %copy-done.15, bf16[512,256]{1,0:T(8,128)(2,1)S(1)} %copy-done.13, ...), kind=kOutput, calls=%fused_computation.1 | convolution fusion | flops 2460745728 | bytes 8650752 | tf_op jit(solution)/shard_map/dot_general | solution.py:26
  366.5 2.8 collective-permute-start.118
  382.7 13.2 %collective-permute-done.100 = f32[3,256]{1,0:T(4,128)S(1)} collective-permute-done((f32[3,256]{1,0:T(4,128)S(1)}, f32[3,256]{1,0:T(4,128)S(1)}, u32[]{:S(2)}, u32[]{:S(2)}) %collective-permute-start.100) | collective-permute-done | bytes 3104 | tf_op jit(solution)/shard_map/ppermute | solution.py:35
  396.8 3.6 collective-permute-done.101
  401.4 5.0 collective-permute-done.103
  406.8 3.0 collective-permute-start.104
  409.9 14.9 %collective-permute-done.104 = bf16[32,1024]{1,0:T(8,128)(2,1)S(1)} collective-permute-done((bf16[32,1024]{1,0:T(8,128)(2,1)S(1)}, bf16[32,1024]{1,0:T(8,128)(2,1)S(1)}, u32[]{:S(2)}, u32[]{:S(2)}) %collective-permute-start.104) | collective-permute-done | bytes 65568 | tf_op jit(solution)/shard_map/ppermute | solution.py:35
  425.8 3.4 collective-permute-start.105
  431.8 3.0 collective-permute-start.94
  435.4 25.1 %collective-permute-done.94 = bf16[256,768]{1,0:T(8,128)(2,1)S(1)} collective-permute-done((bf16[256,768]{1,0:T(8,128)(2,1)S(1)}, bf16[256,768]{1,0:T(8,128)(2,1)S(1)}, u32[]{:S(2)}, u32[]{:S(2)}) %collective-permute-start.94) | collective-permute-done | bytes 393248 | tf_op jit(solution)/shard_map/ppermute | solution.py:35
  460.5 3.6 collective-permute-start.106
  464.9 5.9 %collective-permute-done.95 = bf16[128,768]{1,0:T(8,128)(2,1)S(1)} collective-permute-done((bf16[128,768]{1,0:T(8,128)(2,1)S(1)}, bf16[128,768]{1,0:T(8,128)(2,1)S(1)}, u32[]{:S(2)}, u32[]{:S(2)}) %collective-permute-start.95) | collective-permute-done | bytes 196640 | tf_op jit(solution)/shard_map/ppermute | solution.py:35
  473.1 3.9 collective-permute-done.96
  481.0 10.8 %collective-permute-done.97 = bf16[256,768]{1,0:T(8,128)(2,1)S(1)} collective-permute-done((bf16[256,768]{1,0:T(8,128)(2,1)S(1)}, bf16[256,768]{1,0:T(8,128)(2,1)S(1)}, u32[]{:S(2)}, u32[]{:S(2)}) %collective-permute-start.97) | collective-permute-done | bytes 393248 | tf_op jit(solution)/shard_map/ppermute | solution.py:35
  498.1 11.6 %collective-permute-done.98 = bf16[512,768]{1,0:T(8,128)(2,1)S(1)} collective-permute-done((bf16[512,768]{1,0:T(8,128)(2,1)S(1)}, bf16[512,768]{1,0:T(8,128)(2,1)S(1)}, u32[]{:S(2)}, u32[]{:S(2)}) %collective-permute-start.98) | collective-permute-done | bytes 786464 | tf_op jit(solution)/shard_map/ppermute | solution.py:35
  (722 shorter events, 220.4 us)
Async XLA Ops:
  4.8 22.7 %collective-permute-start.8 = (bf16[6,256]{1,0:T(8,128)(2,1)S(1)}, bf16[6,256]{1,0:T(8,128)(2,1)}, u32[]{:S(2)}, u32[]{:S(2)}) collective-permute-start(bf16[6,256]{1,0:T(8,128)(2,1)S(1)} %stack.36), channel_id=1, source_target_pairs={{0,1},{1,0},{2,3},{3,2},{4,5},{5,4},{6,7},{7,6},{8,9},{9,8},{10,11... | collective-permute-start | bytes 9224 | tf_op jit(solution)/shard_map/ppermute | solution.py:35
  5.4 17.8 %collective-permute-start.6 = (bf16[6,256]{1,0:T(8,128)(2,1)S(1)}, bf16[6,256]{1,0:T(8,128)(2,1)}, u32[]{:S(2)}, u32[]{:S(2)}) collective-permute-start(bf16[6,256]{1,0:T(8,128)(2,1)S(1)} %stack.36), channel_id=1, source_target_pairs={{0,2},{1,3},{2,0},{3,1},{4,6},{5,7},{6,4},{7,5},{8,10},{9,11},{10,... | collective-permute-start | bytes 9224 | tf_op jit(solution)/shard_map/ppermute | solution.py:35
  9.6 26.4 %collective-permute-start.35 = (bf16[512,256]{1,0:T(8,128)(2,1)}, bf16[512,256]{1,0:T(8,128)(2,1)}, u32[]{:S(2)}, u32[]{:S(2)}) collective-permute-start(bf16[512,256]{1,0:T(8,128)(2,1)} %slice.97), channel_id=1, source_target_pairs={{0,1},{1,0},{2,3},{3,2},{4,5},{5,4},{6,7},{7,6},{8,9},{9,8},{10,11... | collective-permute-start | bytes 786440 | tf_op jit(solution)/shard_map/ppermute | solution.py:35
  9.8 20.8 %collective-permute-start.33 = (bf16[512,256]{1,0:T(8,128)(2,1)}, bf16[512,256]{1,0:T(8,128)(2,1)}, u32[]{:S(2)}, u32[]{:S(2)}) collective-permute-start(bf16[512,256]{1,0:T(8,128)(2,1)} %slice.97), channel_id=1, source_target_pairs={{0,2},{1,3},{2,0},{3,1},{4,6},{5,7},{6,4},{7,5},{8,10},{9,11},{10,... | collective-permute-start | bytes 786440 | tf_op jit(solution)/shard_map/ppermute | solution.py:35
  11.9 19.7 %collective-permute-start.80 = (bf16[128,256]{1,0:T(8,128)(2,1)}, bf16[128,256]{1,0:T(8,128)(2,1)S(1)}, u32[]{:S(2)}, u32[]{:S(2)}) collective-permute-start(bf16[128,256]{1,0:T(8,128)(2,1)} %get-tuple-element.235), channel_id=1, source_target_pairs={{0,1},{1,0},{2,3},{3,2},{4,5},{5,4},{6,7},{7,6},{8,9},{9,8},{10,11... | collective-permute-start | bytes 196616 | tf_op jit(solution)/shard_map/ppermute | solution.py:35
  41.5 14.5 %collective-permute-start.18 = (bf16[512,256]{1,0:T(8,128)(2,1)}, bf16[512,256]{1,0:T(8,128)(2,1)}, u32[]{:S(2)}, u32[]{:S(2)}) collective-permute-start(bf16[512,256]{1,0:T(8,128)(2,1)} %get-tuple-element.187), channel_id=1, source_target_pairs={{0,2},{1,3},{2,0},{3,1},{4,6},{5,7},{6,4},{7,5},{8,10},{9,11},{10,... | collective-permute-start | bytes 786440 | tf_op jit(solution)/shard_map/ppermute | solution.py:35
  45.5 17.0 %collective-permute-start.2 = (bf16[512,256]{1,0:T(8,128)(2,1)}, bf16[512,256]{1,0:T(8,128)(2,1)S(1)}, u32[]{:S(2)}, u32[]{:S(2)}) collective-permute-start(bf16[512,256]{1,0:T(8,128)(2,1)} %get-tuple-element.186), channel_id=1, source_target_pairs={{0,1},{1,0},{2,3},{3,2},{4,5},{5,4},{6,7},{7,6},{8,9},{9,8},{10,11... | collective-permute-start | bytes 786440 | tf_op jit(solution)/shard_map/ppermute | solution.py:35
  45.6 16.9 %collective-permute-start.20 = (bf16[512,256]{1,0:T(8,128)(2,1)}, bf16[512,256]{1,0:T(8,128)(2,1)S(1)}, u32[]{:S(2)}, u32[]{:S(2)}) collective-permute-start(bf16[512,256]{1,0:T(8,128)(2,1)} %get-tuple-element.187), channel_id=1, source_target_pairs={{0,1},{1,0},{2,3},{3,2},{4,5},{5,4},{6,7},{7,6},{8,9},{9,8},{10,11... | collective-permute-start | bytes 786440 | tf_op jit(solution)/shard_map/ppermute | solution.py:35
  50.3 12.2 %collective-permute-start.1 = (bf16[512,256]{1,0:T(8,128)(2,1)}, bf16[512,256]{1,0:T(8,128)(2,1)}, u32[]{:S(2)}, u32[]{:S(2)}) collective-permute-start(bf16[512,256]{1,0:T(8,128)(2,1)} %collective-permute-done), channel_id=1, source_target_pairs={{0,1},{1,0},{2,3},{3,2},{4,5},{5,4},{6,7},{7,6},{8,9},{9,8},{10,11... | collective-permute-start | bytes 786440 | tf_op jit(solution)/shard_map/ppermute | solution.py:35
  100.6 13.6 %collective-permute-start.23 = (bf16[128,1024]{1,0:T(8,128)(2,1)S(1)}, bf16[128,1024]{1,0:T(8,128)(2,1)S(1)}, u32[]{:S(2)}, u32[]{:S(2)}) collective-permute-start(bf16[128,1024]{1,0:T(8,128)(2,1)S(1)} %add_convert_fusion.19), channel_id=1, source_target_pairs={{0,2},{1,3},{2,0},{3,1},{4,6},{5,7},{6,4},{7,5},{8,10},{9,11},{10,... | collective-permute-start | bytes 786440 | tf_op jit(solution)/shard_map/ppermute | solution.py:35
  101.7 17.6 %collective-permute-start.5 = (bf16[128,1024]{1,0:T(8,128)(2,1)S(1)}, bf16[128,1024]{1,0:T(8,128)(2,1)S(1)}, u32[]{:S(2)}, u32[]{:S(2)}) collective-permute-start(bf16[128,1024]{1,0:T(8,128)(2,1)S(1)} %add_convert_fusion.22), channel_id=1, source_target_pairs={{0,2},{1,3},{2,0},{3,1},{4,6},{5,7},{6,4},{7,5},{8,10},{9,11},{10,... | collective-permute-start | bytes 786440 | tf_op jit(solution)/shard_map/ppermute | solution.py:35
  153.5 16.5 %collective-permute-start.42 = (bf16[128,1024]{1,0:T(8,128)(2,1)S(1)}, bf16[128,1024]{1,0:T(8,128)(2,1)S(1)}, u32[]{:S(2)}, u32[]{:S(2)}) collective-permute-start(bf16[128,1024]{1,0:T(8,128)(2,1)S(1)} %get-tuple-element.169), channel_id=1, source_target_pairs={{0,1},{1,0},{2,3},{3,2},{4,5},{5,4},{6,7},{7,6},{8,9},{9,8},{10,11... | collective-permute-start | bytes 786440 | tf_op jit(solution)/shard_map/ppermute | solution.py:35
  157.6 12.5 %collective-permute-start.27 = (bf16[128,1024]{1,0:T(8,128)(2,1)S(1)}, bf16[128,1024]{1,0:T(8,128)(2,1)S(1)}, u32[]{:S(2)}, u32[]{:S(2)}) collective-permute-start(bf16[128,1024]{1,0:T(8,128)(2,1)S(1)} %get-tuple-element.173), channel_id=1, source_target_pairs={{0,1},{1,0},{2,3},{3,2},{4,5},{5,4},{6,7},{7,6},{8,9},{9,8},{10,11... | collective-permute-start | bytes 786440 | tf_op jit(solution)/shard_map/ppermute | solution.py:35
  159.7 14.3 %collective-permute-start.44 = (bf16[128,1024]{1,0:T(8,128)(2,1)S(1)}, bf16[128,1024]{1,0:T(8,128)(2,1)S(1)}, u32[]{:S(2)}, u32[]{:S(2)}) collective-permute-start(bf16[128,1024]{1,0:T(8,128)(2,1)S(1)} %add_convert_fusion.15), channel_id=1, source_target_pairs={{0,2},{1,3},{2,0},{3,1},{4,6},{5,7},{6,4},{7,5},{8,10},{9,11},{10,... | collective-permute-start | bytes 786440 | tf_op jit(solution)/shard_map/ppermute | solution.py:35
  161.5 18.2 %collective-permute-start.29 = (bf16[128,1024]{1,0:T(8,128)(2,1)S(1)}, bf16[128,1024]{1,0:T(8,128)(2,1)S(1)}, u32[]{:S(2)}, u32[]{:S(2)}) collective-permute-start(bf16[128,1024]{1,0:T(8,128)(2,1)S(1)} %add_convert_fusion.18), channel_id=1, source_target_pairs={{0,2},{1,3},{2,0},{3,1},{4,6},{5,7},{6,4},{7,5},{8,10},{9,11},{10,... | collective-permute-start | bytes 786440 | tf_op jit(solution)/shard_map/ppermute | solution.py:35
  169.6 26.3 %collective-permute-start.52 = (bf16[128,1024]{1,0:T(8,128)(2,1)S(1)}, bf16[128,1024]{1,0:T(8,128)(2,1)S(1)}, u32[]{:S(2)}, u32[]{:S(2)}) collective-permute-start(bf16[128,1024]{1,0:T(8,128)(2,1)S(1)} %get-tuple-element.57), channel_id=1, source_target_pairs={{0,2},{1,3},{2,0},{3,1},{4,6},{5,7},{6,4},{7,5},{8,10},{9,11},{10,... | collective-permute-start | bytes 786440 | tf_op jit(solution)/shard_map/ppermute | solution.py:35
  170.1 26.5 %collective-permute-start.51 = (bf16[128,1024]{1,0:T(8,128)(2,1)S(1)}, bf16[128,1024]{1,0:T(8,128)(2,1)S(1)}, u32[]{:S(2)}, u32[]{:S(2)}) collective-permute-start(bf16[128,1024]{1,0:T(8,128)(2,1)S(1)} %get-tuple-element.57), channel_id=1, source_target_pairs={{0,1},{1,0},{2,3},{3,2},{4,5},{5,4},{6,7},{7,6},{8,9},{9,8},{10,11... | collective-permute-start | bytes 786440 | tf_op jit(solution)/shard_map/ppermute | solution.py:35
  214.0 23.7 %collective-permute-start.54 = (bf16[128,1024]{1,0:T(8,128)(2,1)S(1)}, bf16[128,1024]{1,0:T(8,128)(2,1)S(1)}, u32[]{:S(2)}, u32[]{:S(2)}) collective-permute-start(bf16[128,1024]{1,0:T(8,128)(2,1)S(1)} %get-tuple-element.167), channel_id=1, source_target_pairs={{0,1},{1,0},{2,3},{3,2},{4,5},{5,4},{6,7},{7,6},{8,9},{9,8},{10,11... | collective-permute-start | bytes 786440 | tf_op jit(solution)/shard_map/ppermute | solution.py:35
  214.7 20.3 %collective-permute-start.69 = (bf16[128,1024]{1,0:T(8,128)(2,1)S(1)}, bf16[128,1024]{1,0:T(8,128)(2,1)S(1)}, u32[]{:S(2)}, u32[]{:S(2)}) collective-permute-start(bf16[128,1024]{1,0:T(8,128)(2,1)S(1)} %get-tuple-element.165), channel_id=1, source_target_pairs={{0,1},{1,0},{2,3},{3,2},{4,5},{5,4},{6,7},{7,6},{8,9},{9,8},{10,11... | collective-permute-start | bytes 786440 | tf_op jit(solution)/shard_map/ppermute | solution.py:35
  216.9 19.3 %collective-permute-start.71 = (bf16[128,1024]{1,0:T(8,128)(2,1)S(1)}, bf16[128,1024]{1,0:T(8,128)(2,1)S(1)}, u32[]{:S(2)}, u32[]{:S(2)}) collective-permute-start(bf16[128,1024]{1,0:T(8,128)(2,1)S(1)} %add_convert_fusion.10), channel_id=1, source_target_pairs={{0,2},{1,3},{2,0},{3,1},{4,6},{5,7},{6,4},{7,5},{8,10},{9,11},{10,... | collective-permute-start | bytes 786440 | tf_op jit(solution)/shard_map/ppermute | solution.py:35
  252.9 33.3 %collective-permute-start.114 = (bf16[512,1024]{1,0:T(8,128)(2,1)S(1)}, bf16[512,1024]{1,0:T(8,128)(2,1)S(1)}, u32[]{:S(2)}, u32[]{:S(2)}) collective-permute-start(bf16[512,1024]{1,0:T(8,128)(2,1)S(1)} %dynamic-slice_convert_fusion.1), channel_id=1, source_target_pairs={{0,8},{4,12},{8,0},{12,4},{16,24},{20,28},{24,16},{28,20},{1,9},{5... | collective-permute-start | bytes 3145736 | tf_op jit(solution)/shard_map/ppermute | solution.py:35
  254.6 22.5 %collective-permute-start.112 = (f32[10,256]{1,0:T(8,128)S(1)}, f32[10,256]{1,0:T(8,128)S(1)}, u32[]{:S(2)}, u32[]{:S(2)}) collective-permute-start(f32[10,256]{1,0:T(8,128)S(1)} %fusion.157), channel_id=1, source_target_pairs={{0,8},{4,12},{8,0},{12,4},{16,24},{20,28},{24,16},{28,20},{1,9},{5... | collective-permute-start | bytes 30728 | tf_op jit(solution)/shard_map/ppermute | solution.py:35
  256.9 31.1 %collective-permute-start.120 = (bf16[512,1024]{1,0:T(8,128)(2,1)S(1)}, bf16[512,1024]{1,0:T(8,128)(2,1)S(1)}, u32[]{:S(2)}, u32[]{:S(2)}) collective-permute-start(bf16[512,1024]{1,0:T(8,128)(2,1)S(1)} %dynamic-slice_convert_fusion), channel_id=1, source_target_pairs={{0,4},{4,0},{8,12},{12,8},{16,20},{20,16},{24,28},{28,24},{1,5},{5... | collective-permute-start | bytes 3145736 | tf_op jit(solution)/shard_map/ppermute | solution.py:35
  287.6 26.9 %collective-permute-start.115 = (bf16[256,1024]{1,0:T(8,128)(2,1)}, bf16[256,1024]{1,0:T(8,128)(2,1)}, u32[]{:S(2)}, u32[]{:S(2)}) collective-permute-start(bf16[256,1024]{1,0:T(8,128)(2,1)} %dynamic-slice_convert_fusion.4), channel_id=1, source_target_pairs={{0,16},{4,20},{8,24},{12,28},{16,0},{20,4},{24,8},{28,12},{1,17},{... | collective-permute-start | bytes 1572872 | tf_op jit(solution)/shard_map/ppermute | solution.py:35
  290.6 15.4 %collective-permute-start.73 = (bf16[128,1024]{1,0:T(8,128)(2,1)S(1)}, bf16[128,1024]{1,0:T(8,128)(2,1)S(1)}, u32[]{:S(2)}, u32[]{:S(2)}) collective-permute-start(bf16[128,1024]{1,0:T(8,128)(2,1)S(1)} %get-tuple-element.74), channel_id=1, source_target_pairs={{0,2},{1,3},{2,0},{3,1},{4,6},{5,7},{6,4},{7,5},{8,10},{9,11},{10,... | collective-permute-start | bytes 786440 | tf_op jit(solution)/shard_map/ppermute | solution.py:35
  303.5 22.1 %collective-permute-start.121 = (bf16[256,1024]{1,0:T(8,128)(2,1)}, bf16[256,1024]{1,0:T(8,128)(2,1)}, u32[]{:S(2)}, u32[]{:S(2)}) collective-permute-start(bf16[256,1024]{1,0:T(8,128)(2,1)} %dynamic-slice_convert_fusion.3), channel_id=1, source_target_pairs={{0,8},{4,12},{8,0},{12,4},{16,24},{20,28},{24,16},{28,20},{1,9},{5... | collective-permute-start | bytes 1572872 | tf_op jit(solution)/shard_map/ppermute | solution.py:35
  306.0 22.1 %collective-permute-start.60 = (bf16[512,256]{1,0:T(8,128)(2,1)}, bf16[512,256]{1,0:T(8,128)(2,1)}, u32[]{:S(2)}, u32[]{:S(2)}) collective-permute-start(bf16[512,256]{1,0:T(8,128)(2,1)} %get-tuple-element.149), channel_id=1, source_target_pairs={{0,1},{1,0},{2,3},{3,2},{4,5},{5,4},{6,7},{7,6},{8,9},{9,8},{10,11... | collective-permute-start | bytes 786440 | tf_op jit(solution)/shard_map/ppermute | solution.py:35
  307.4 20.7 %collective-permute-start.62 = (bf16[512,256]{1,0:T(8,128)(2,1)}, bf16[512,256]{1,0:T(8,128)(2,1)}, u32[]{:S(2)}, u32[]{:S(2)}) collective-permute-start(bf16[512,256]{1,0:T(8,128)(2,1)} %add_convert_fusion.12), channel_id=1, source_target_pairs={{0,2},{1,3},{2,0},{3,1},{4,6},{5,7},{6,4},{7,5},{8,10},{9,11},{10,... | collective-permute-start | bytes 786440 | tf_op jit(solution)/shard_map/ppermute | solution.py:35
  311.5 31.8 %collective-permute-start.88 = (bf16[128,1024]{1,0:T(8,128)(2,1)}, bf16[128,1024]{1,0:T(8,128)(2,1)}, u32[]{:S(2)}, u32[]{:S(2)}) collective-permute-start(bf16[128,1024]{1,0:T(8,128)(2,1)} %get-tuple-element.72), channel_id=1, source_target_pairs={{0,2},{1,3},{2,0},{3,1},{4,6},{5,7},{6,4},{7,5},{8,10},{9,11},{10,... | collective-permute-start | bytes 786440 | tf_op jit(solution)/shard_map/ppermute | solution.py:35
  314.5 29.7 %collective-permute-start.87 = (bf16[128,1024]{1,0:T(8,128)(2,1)}, bf16[128,1024]{1,0:T(8,128)(2,1)}, u32[]{:S(2)}, u32[]{:S(2)}) collective-permute-start(bf16[128,1024]{1,0:T(8,128)(2,1)} %get-tuple-element.72), channel_id=1, source_target_pairs={{0,1},{1,0},{2,3},{3,2},{4,5},{5,4},{6,7},{7,6},{8,9},{9,8},{10,11... | collective-permute-start | bytes 786440 | tf_op jit(solution)/shard_map/ppermute | solution.py:35
  328.1 13.6 %collective-permute-start.122 = (bf16[128,1024]{1,0:T(8,128)(2,1)S(1)}, bf16[128,1024]{1,0:T(8,128)(2,1)S(1)}, u32[]{:S(2)}, u32[]{:S(2)}) collective-permute-start(bf16[128,1024]{1,0:T(8,128)(2,1)S(1)} %dynamic-slice_convert_fusion.6), channel_id=1, source_target_pairs={{0,16},{4,20},{8,24},{12,28},{16,0},{20,4},{24,8},{28,12},{1,17},{... | collective-permute-start | bytes 786440 | tf_op jit(solution)/shard_map/ppermute | solution.py:35
  328.1 48.3 %collective-permute-start.75 = (bf16[512,256]{1,0:T(8,128)(2,1)}, bf16[512,256]{1,0:T(8,128)(2,1)}, u32[]{:S(2)}, u32[]{:S(2)}) collective-permute-start(bf16[512,256]{1,0:T(8,128)(2,1)} %get-tuple-element.155), channel_id=1, source_target_pairs={{0,1},{1,0},{2,3},{3,2},{4,5},{5,4},{6,7},{7,6},{8,9},{9,8},{10,11... | collective-permute-start | bytes 786440 | tf_op jit(solution)/shard_map/ppermute | solution.py:35
  341.8 22.8 %collective-permute-start.117 = (bf16[128,1024]{1,0:T(8,128)(2,1)}, bf16[128,1024]{1,0:T(8,128)(2,1)}, u32[]{:S(2)}, u32[]{:S(2)}) collective-permute-start(bf16[128,1024]{1,0:T(8,128)(2,1)} %add_convert_fusion.4), channel_id=1, source_target_pairs={{0,4},{4,0},{8,12},{12,8},{16,20},{20,16},{24,28},{28,24},{1,5},{5... | collective-permute-start | bytes 786440 | tf_op jit(solution)/shard_map/ppermute | solution.py:35
  343.2 27.1 %collective-permute-start.123 = (bf16[128,1024]{1,0:T(8,128)(2,1)S(1)}, bf16[128,1024]{1,0:T(8,128)(2,1)}, u32[]{:S(2)}, u32[]{:S(2)}) collective-permute-start(bf16[128,1024]{1,0:T(8,128)(2,1)S(1)} %add_convert_fusion.3), channel_id=1, source_target_pairs={{0,16},{4,20},{8,24},{12,28},{16,0},{20,4},{24,8},{28,12},{1,17},{... | collective-permute-start | bytes 786440 | tf_op jit(solution)/shard_map/ppermute | solution.py:35
  344.2 33.7 %collective-permute-start.77 = (bf16[512,256]{1,0:T(8,128)(2,1)}, bf16[512,256]{1,0:T(8,128)(2,1)}, u32[]{:S(2)}, u32[]{:S(2)}) collective-permute-start(bf16[512,256]{1,0:T(8,128)(2,1)} %add_convert_fusion.9), channel_id=1, source_target_pairs={{0,2},{1,3},{2,0},{3,1},{4,6},{5,7},{6,4},{7,5},{8,10},{9,11},{10,... | collective-permute-start | bytes 786440 | tf_op jit(solution)/shard_map/ppermute | solution.py:35
  366.5 59.4 %collective-permute-start.118 = (bf16[256,1024]{1,0:T(8,128)(2,1)}, bf16[256,1024]{1,0:T(8,128)(2,1)S(1)}, u32[]{:S(2)}, u32[]{:S(2)}) collective-permute-start(bf16[256,1024]{1,0:T(8,128)(2,1)} %pad_maximum_fusion.13), channel_id=1, source_target_pairs={{0,16},{4,20},{8,24},{12,28},{16,0},{20,4},{24,8},{28,12},{1,17},{... | collective-permute-start | bytes 1572872 | tf_op jit(solution)/shard_map/ppermute | solution.py:35
  372.5 57.2 %collective-permute-start.124 = (bf16[256,1024]{1,0:T(8,128)(2,1)}, bf16[256,1024]{1,0:T(8,128)(2,1)}, u32[]{:S(2)}, u32[]{:S(2)}) collective-permute-start(bf16[256,1024]{1,0:T(8,128)(2,1)} %pad_maximum_fusion.14), channel_id=1, source_target_pairs={{0,8},{4,12},{8,0},{12,4},{16,24},{20,28},{24,16},{28,20},{1,9},{5... | collective-permute-start | bytes 1572872 | tf_op jit(solution)/shard_map/ppermute | solution.py:35
  376.5 23.9 %collective-permute-start.102 = (bf16[128,1024]{1,0:T(8,128)(2,1)S(1)}, bf16[128,1024]{1,0:T(8,128)(2,1)S(1)}, u32[]{:S(2)}, u32[]{:S(2)}) collective-permute-start(bf16[128,1024]{1,0:T(8,128)(2,1)S(1)} %dynamic-slice_convert_fusion.8), channel_id=1, source_target_pairs={{0,4},{4,0},{8,12},{12,8},{16,20},{20,16},{24,28},{28,24},{1,5},{5... | collective-permute-start | bytes 786440 | tf_op jit(solution)/shard_map/ppermute | solution.py:35
  378.0 86.3 %collective-permute-start.90 = (bf16[512,256]{1,0:T(8,128)(2,1)S(1)}, bf16[512,256]{1,0:T(8,128)(2,1)S(1)}, u32[]{:S(2)}, u32[]{:S(2)}) collective-permute-start(bf16[512,256]{1,0:T(8,128)(2,1)S(1)} %get-tuple-element.161), channel_id=1, source_target_pairs={{0,1},{1,0},{2,3},{3,2},{4,5},{5,4},{6,7},{7,6},{8,9},{9,8},{10,11... | collective-permute-start | bytes 786440 | tf_op jit(solution)/shard_map/ppermute | solution.py:35
  380.5 15.3 %collective-permute-start.100 = (f32[3,256]{1,0:T(4,128)S(1)}, f32[3,256]{1,0:T(4,128)S(1)}, u32[]{:S(2)}, u32[]{:S(2)}) collective-permute-start(f32[3,256]{1,0:T(4,128)S(1)} %add.821), channel_id=1, source_target_pairs={{0,8},{4,12},{8,0},{12,4},{16,24},{20,28},{24,16},{28,20},{1,9},{5... | collective-permute-start | bytes 9224 | tf_op jit(solution)/shard_map/ppermute | solution.py:35
  406.5 25.1 %collective-permute-start.93 = (bf16[512,768]{1,0:T(8,128)(2,1)S(1)}, bf16[512,768]{1,0:T(8,128)(2,1)S(1)}, u32[]{:S(2)}, u32[]{:S(2)}) collective-permute-start(bf16[512,768]{1,0:T(8,128)(2,1)S(1)} %dynamic-slice_convert_fusion.2), channel_id=1, source_target_pairs={{0,8},{4,12},{8,0},{12,4},{16,24},{20,28},{24,16},{28,20},{1,9},{5... | collective-permute-start | bytes 2359304 | tf_op jit(solution)/shard_map/ppermute | solution.py:35
  406.8 17.9 %collective-permute-start.104 = (bf16[32,1024]{1,0:T(8,128)(2,1)S(1)}, bf16[32,1024]{1,0:T(8,128)(2,1)S(1)}, u32[]{:S(2)}, u32[]{:S(2)}) collective-permute-start(bf16[32,1024]{1,0:T(8,128)(2,1)S(1)} %dynamic-slice_convert_fusion.11), channel_id=1, source_target_pairs={{0,16},{4,20},{8,24},{12,28},{16,0},{20,4},{24,8},{28,12},{1,17},{... | collective-permute-start | bytes 196616 | tf_op jit(solution)/shard_map/ppermute | solution.py:35
  424.8 40.0 %collective-permute-start.92 = (bf16[512,256]{1,0:T(8,128)(2,1)S(1)}, bf16[512,256]{1,0:T(8,128)(2,1)S(1)}, u32[]{:S(2)}, u32[]{:S(2)}) collective-permute-start(bf16[512,256]{1,0:T(8,128)(2,1)S(1)} %add_convert_fusion.6), channel_id=1, source_target_pairs={{0,2},{1,3},{2,0},{3,1},{4,6},{5,7},{6,4},{7,5},{8,10},{9,11},{10,... | collective-permute-start | bytes 786440 | tf_op jit(solution)/shard_map/ppermute | solution.py:35
  429.6 65.5 %collective-permute-start.119 = (bf16[512,1024]{1,0:T(8,128)(2,1)S(1)}, bf16[512,1024]{1,0:T(8,128)(2,1)S(1)}, u32[]{:S(2)}, u32[]{:S(2)}) collective-permute-start(bf16[512,1024]{1,0:T(8,128)(2,1)S(1)} %pad_maximum_fusion.8), channel_id=1, source_target_pairs={{0,8},{4,12},{8,0},{12,4},{16,24},{20,28},{24,16},{28,20},{1,9},{5... | collective-permute-start | bytes 3145736 | tf_op jit(solution)/shard_map/ppermute | solution.py:35
  431.8 28.7 %collective-permute-start.94 = (bf16[256,768]{1,0:T(8,128)(2,1)S(1)}, bf16[256,768]{1,0:T(8,128)(2,1)S(1)}, u32[]{:S(2)}, u32[]{:S(2)}) collective-permute-start(bf16[256,768]{1,0:T(8,128)(2,1)S(1)} %dynamic-slice_convert_fusion.5), channel_id=1, source_target_pairs={{0,16},{4,20},{8,24},{12,28},{16,0},{20,4},{24,8},{28,12},{1,17},{... | collective-permute-start | bytes 1179656 | tf_op jit(solution)/shard_map/ppermute | solution.py:35
  434.9 57.3 %collective-permute-start.125 = (bf16[512,1024]{1,0:T(8,128)(2,1)S(1)}, bf16[512,1024]{1,0:T(8,128)(2,1)S(1)}, u32[]{:S(2)}, u32[]{:S(2)}) collective-permute-start(bf16[512,1024]{1,0:T(8,128)(2,1)S(1)} %pad_maximum_fusion.9), channel_id=1, source_target_pairs={{0,4},{4,0},{8,12},{12,8},{16,20},{20,16},{24,28},{28,24},{1,5},{5... | collective-permute-start | bytes 3145736 | tf_op jit(solution)/shard_map/ppermute | solution.py:35
  477.1 14.8 %collective-permute-start.97 = (bf16[256,768]{1,0:T(8,128)(2,1)S(1)}, bf16[256,768]{1,0:T(8,128)(2,1)S(1)}, u32[]{:S(2)}, u32[]{:S(2)}) collective-permute-start(bf16[256,768]{1,0:T(8,128)(2,1)S(1)} %pad_maximum_fusion.15), channel_id=1, source_target_pairs={{0,16},{4,20},{8,24},{12,28},{16,0},{20,4},{24,8},{28,12},{1,17},{... | collective-permute-start | bytes 1179656 | tf_op jit(solution)/shard_map/ppermute | solution.py:35
  492.1 17.7 %collective-permute-start.98 = (bf16[512,768]{1,0:T(8,128)(2,1)S(1)}, bf16[512,768]{1,0:T(8,128)(2,1)S(1)}, u32[]{:S(2)}, u32[]{:S(2)}) collective-permute-start(bf16[512,768]{1,0:T(8,128)(2,1)S(1)} %pad_maximum_fusion.12), channel_id=1, source_target_pairs={{0,8},{4,12},{8,0},{12,4},{16,24},{20,28},{24,16},{28,20},{1,9},{5... | collective-permute-start | bytes 2359304 | tf_op jit(solution)/shard_map/ppermute | solution.py:35
  (195 other events, 1435.3 us)
